TPU v7x, 32 devices: a whole 2x2x4 slice. The times are simulated.
32 devices in a mesh: dp: 4 (over x, y), ep: 8 (over z, core).
Axes of the slice: x: 2, y: 2, z: 4, core: 2. Of those that a mesh axis runs over, the one named last changes fastest.
Arguments:
- x_in: bfloat16 [131072, 320], P(('dp', 'ep')), parts along dimension 0
- d_out: bfloat16 [131072, 320], P(('dp', 'ep')), parts along dimension 0
- idx_a: int32 [131072, 1], P(('dp', 'ep')), parts along dimension 0
- gate_a: float32 [131072, 1], P(('dp', 'ep')), parts along dimension 0
- idx_b: int32 [131072, 1], P(('dp', 'ep')), parts along dimension 0
- gate_b: float32 [131072, 1], P(('dp', 'ep')), parts along dimension 0
- w1_a: bfloat16 [16, 320, 512], P('ep')
- w3_a: bfloat16 [16, 320, 512], P('ep')
- w2_a: bfloat16 [16, 512, 320], P('ep')
- ws1_a: bfloat16 [320, 512], replicated
- ws3_a: bfloat16 [320, 512], replicated
- ws2_a: bfloat16 [512, 320], replicated
- w1_b: bfloat16 [16, 320, 512], P('ep')
- w3_b: bfloat16 [16, 320, 512], P('ep')
- w2_b: bfloat16 [16, 512, 320], P('ep')
- ws1_b: bfloat16 [320, 512], replicated
- ws3_b: bfloat16 [320, 512], replicated
- ws2_b: bfloat16 [512, 320], replicated
Outputs:
- output 1: bfloat16 [131072, 320], P(('dp', 'ep')), parts along dimension 0
- output 2: bfloat16 [131072, 320], P(('dp', 'ep')), parts along dimension 0
- output 3: float32 [64, 320, 512], P(('dp', 'ep')), parts along dimension 0
- output 4: float32 [64, 320, 512], P(('dp', 'ep')), parts along dimension 0
- output 5: float32 [64, 512, 320], P(('dp', 'ep')), parts along dimension 0
- output 6: float32 [64, 320, 512], P(('dp', 'ep')), parts along dimension 0
- output 7: float32 [64, 320, 512], P(('dp', 'ep')), parts along dimension 0
- output 8: float32 [64, 512, 320], P(('dp', 'ep')), parts along dimension 0
- output 9: float32 [131072, 1], P(('dp', 'ep')), parts along dimension 0
- output 10: float32 [131072, 1], P(('dp', 'ep')), parts along dimension 0
There are 4 independent parts. A program takes and returns all parts, laid end to end along the dimension named above; an argument that names none is the same for every part.
All inputs are finite; a program needn't handle non-finite values.
Results may differ from a plain program's by a relative error of at most 0.00549.
Values are sent between devices in bfloat16 or wider.
A program may use at most 1 GiB of HBM per device.

v0:
```python
import jax
import jax.numpy as jnp
from jax import lax
from jax.sharding import PartitionSpec as P


def slot_capacity(tokens, n_experts, top_k):
    return top_k * ((2 * tokens + n_experts - 1) // n_experts)


def route_tables(expert_ids, n_experts, capacity):
    flat_ids = expert_ids.reshape(-1)
    pair_count = flat_ids.shape[0]
    pair_order = jnp.argsort(flat_ids, stable=True)
    expert_count = jax.ops.segment_sum(jnp.ones_like(flat_ids), flat_ids, num_segments=n_experts)
    expert_start = jnp.cumsum(expert_count) - expert_count
    position = flat_ids * capacity + jnp.argsort(pair_order) - expert_start[flat_ids]
    slot_index = jnp.arange(capacity)
    src_pair = pair_order[jnp.minimum(expert_start[:, None] + slot_index[None, :], pair_count - 1)]
    slot_used = slot_index[None, :] < expert_count[:, None]
    return src_pair.reshape(-1), slot_used.reshape(-1), position


def to_experts(rows, group_size, capacity):
    n_local = rows.shape[0] // (group_size * capacity)
    row_shape = rows.shape[1:]
    shaped = rows.reshape((group_size, n_local, capacity) + row_shape)
    received = lax.all_to_all(shaped, 'ep', 0, 2, tiled=True)
    return received.reshape((n_local, group_size * capacity) + row_shape)


def to_sources(rows, group_size, capacity):
    n_local = rows.shape[0]
    row_shape = rows.shape[2:]
    shaped = rows.reshape((1, n_local, group_size * capacity) + row_shape)
    received = lax.all_to_all(shaped, 'ep', 2, 0, tiled=True)
    return received.reshape((group_size * n_local * capacity,) + row_shape)


def swiglu_grads(pre_gate, pre_up, d_hidden):
    sigma = jax.nn.sigmoid(pre_gate)
    d_gate = d_hidden * pre_up * sigma * (1.0 + pre_gate * (1.0 - sigma))
    d_up = d_hidden * pre_gate * sigma
    return d_gate.astype(jnp.bfloat16), d_up.astype(jnp.bfloat16)


def expert_hidden(rows, w_gate, w_up):
    pre_gate = jnp.einsum('erd,edf->erf', rows, w_gate, preferred_element_type=jnp.float32)
    pre_up = jnp.einsum('erd,edf->erf', rows, w_up, preferred_element_type=jnp.float32)
    return pre_gate, pre_up, (jax.nn.silu(pre_gate) * pre_up).astype(jnp.bfloat16)


def shared_hidden(rows, s_gate, s_up):
    pre_gate = jnp.dot(rows, s_gate, preferred_element_type=jnp.float32)
    pre_up = jnp.dot(rows, s_up, preferred_element_type=jnp.float32)
    return pre_gate, pre_up, (jax.nn.silu(pre_gate) * pre_up).astype(jnp.bfloat16)


def shared_input_grad(x_rows, d_next, s_gate, s_up, s_down):
    pre = shared_hidden(x_rows, s_gate, s_up)
    projected = jnp.einsum('td,fd->tf', d_next, s_down, preferred_element_type=jnp.float32)
    ds_gate, ds_up = swiglu_grads(pre[0], pre[1], projected)
    return (jnp.einsum('tf,df->td', ds_gate, s_gate, preferred_element_type=jnp.float32)
            + jnp.einsum('tf,df->td', ds_up, s_up, preferred_element_type=jnp.float32))


def send_rows(rows, tables, top_k, group_size, capacity):
    sent = jnp.where(tables[1][:, None], rows[tables[0] // top_k], 0)
    return to_experts(sent, group_size, capacity)


def layer_forward(x_rows, tables, gates, weights, group_size, capacity):
    w_gate, w_up, w_down, s_gate, s_up, s_down = weights
    tokens, top_k = gates.shape
    received = send_rows(x_rows, tables, top_k, group_size, capacity)
    hidden = expert_hidden(received, w_gate, w_up)[2]
    expert_out = jnp.einsum('erf,efd->erd', hidden, w_down,
                            preferred_element_type=jnp.float32).astype(jnp.bfloat16)
    returned = to_sources(expert_out, group_size, capacity)
    per_pair = returned[tables[2]].reshape(tokens, top_k, -1)
    shared = jnp.dot(shared_hidden(x_rows, s_gate, s_up)[2], s_down, preferred_element_type=jnp.float32)
    mixed = x_rows.astype(jnp.float32) + shared + jnp.sum(gates[:, :, None] * per_pair, axis=1)
    return mixed.astype(jnp.bfloat16), received


def layer_backward(x_rows, d_next, tables, gates, weights, received, group_size, capacity):
    w_gate, w_up, w_down, s_gate, s_up, s_down = weights
    tokens, top_k = gates.shape
    src_pair, slot_used, position = tables
    dy_rows = to_experts(jnp.where(slot_used[:, None], d_next[src_pair // top_k], 0), group_size, capacity)
    gate_rows = to_experts(jnp.where(slot_used, gates.reshape(-1)[src_pair], 0.0), group_size, capacity)
    pre_gate, pre_up, hidden = expert_hidden(received, w_gate, w_up)
    projected = jnp.einsum('erd,efd->erf', dy_rows, w_down, preferred_element_type=jnp.float32)
    gate_grad = jnp.sum(hidden.astype(jnp.float32) * projected, axis=2)
    scaled = (gate_rows[:, :, None] * dy_rows).astype(jnp.bfloat16)
    dw_down = jnp.einsum('erf,erd->efd', hidden, scaled, preferred_element_type=jnp.float32)
    da_gate, da_up = swiglu_grads(pre_gate, pre_up, gate_rows[:, :, None] * projected)
    dw_gate = jnp.einsum('erd,erf->edf', received, da_gate, preferred_element_type=jnp.float32)
    dw_up = jnp.einsum('erd,erf->edf', received, da_up, preferred_element_type=jnp.float32)
    d_sent = (jnp.einsum('erf,edf->erd', da_gate, w_gate, preferred_element_type=jnp.float32)
              + jnp.einsum('erf,edf->erd', da_up, w_up, preferred_element_type=jnp.float32)
              ).astype(jnp.bfloat16)
    du_back = to_sources(d_sent, group_size, capacity)
    gate_back = to_sources(gate_grad, group_size, capacity)
    du_pair = du_back[position].reshape(tokens, top_k, -1)
    d_gates = gate_back[position].reshape(tokens, top_k)
    shared_dx = shared_input_grad(x_rows, d_next, s_gate, s_up, s_down)
    d_rows = d_next.astype(jnp.float32) + shared_dx + jnp.sum(du_pair, axis=1, dtype=jnp.float32)
    return d_rows.astype(jnp.bfloat16), dw_gate, dw_up, dw_down, d_gates


def solution(mesh):
    group_size = mesh.shape['ep']
    token_spec = P(('dp', 'ep'), None)
    expert_spec = P('ep', None, None)
    shared_spec = P(None, None)
    grad_spec = P(('dp', 'ep'), None, None)
    layer_specs = (expert_spec,) * 3 + (shared_spec,) * 3

    def device_step(x_in, d_out, idx_a, gate_a, idx_b, gate_b,
                    w1_a, w3_a, w2_a, ws1_a, ws3_a, ws2_a,
                    w1_b, w3_b, w2_b, ws1_b, ws3_b, ws2_b):
        weights_a = (w1_a, w3_a, w2_a, ws1_a, ws3_a, ws2_a)
        weights_b = (w1_b, w3_b, w2_b, ws1_b, ws3_b, ws2_b)
        tokens, top_k = idx_a.shape
        n_experts = w1_a.shape[0] * group_size
        capacity = slot_capacity(tokens, n_experts, top_k)
        tables_a = route_tables(idx_a, n_experts, capacity)
        tables_b = route_tables(idx_b, n_experts, capacity)
        x_mid = layer_forward(x_in, tables_a, gate_a, weights_a, group_size, capacity)[0]
        x_last, kept_b = layer_forward(x_mid, tables_b, gate_b, weights_b, group_size, capacity)
        d_mid, dw1_b, dw3_b, dw2_b, dgate_b = layer_backward(
            x_mid, d_out, tables_b, gate_b, weights_b, kept_b, group_size, capacity)
        resent_a = send_rows(x_in, tables_a, top_k, group_size, capacity)
        d_first, dw1_a, dw3_a, dw2_a, dgate_a = layer_backward(
            x_in, d_mid, tables_a, gate_a, weights_a, resent_a, group_size, capacity)
        return (x_last, d_first, dw1_a, dw3_a, dw2_a, dw1_b, dw3_b, dw2_b, dgate_a, dgate_b)

    in_specs = (token_spec,) * 6 + layer_specs + layer_specs
    out_specs = (token_spec, token_spec) + (grad_spec,) * 6 + (token_spec, token_spec)
    return jax.shard_map(device_step, mesh=mesh, in_specs=in_specs, out_specs=out_specs, check_vma=False)
```

profile of v0, /device:TPU:0, one launch (start us, length us, event | category | flops | bytes accessed | tf_op | source)
XLA Modules:
  0.0 1705.7 jit_solution(9821233463225342200)
XLA Ops:
  11.9 28.9 %scatter_custom_fusion = s32[16]{0:T(128)S(1)} fusion(s32[4096]{0:T(1024)} %bitcast.213, s32[4096]{0:T(1024)S(1)} %broadcast.330, s32[]{:T(128)} %constant.53.clone.1), kind=kCustom, calls=%fused_computation.122 | custom fusion | flops 4096 | bytes 576 | tf_op jit(solution)/shard_map/scatter-add | solution.py:15
  41.2 45.5 %gather_fusion = s32[8192]{0:T(1024)S(1)} fusion(s32[4096]{0:T(1024)S(1)} %get-tuple-element.14, s32[8192]{0:T(1024)S(1)} %broadcast_clamp_fusion.2), kind=kCustom, calls=%fused_computation | custom fusion | bytes 98304 | tf_op jit(solution)/shard_map/gather | solution.py:19
  86.9 34.7 %gather_fusion.1 = bf16[8192,320]{1,0:T(8,128)(2,1)} fusion(bf16[4096,320]{1,0:T(8,128)(2,1)} %copy.133, s32[8192]{0:T(1024)S(1)} %broadcast_clamp_fusion.3), kind=kCustom, calls=%fused_computation.1 | custom fusion | bytes 10518528 | tf_op jit(solution)/shard_map/gather | solution.py:68
  132.8 124.4 %all_to_all.185 = bf16[8,2,512,320]{2,3,1,0:T(8,128)(2,1)S(1)} all-to-all(bf16[8,2,512,320]{2,3,1,0:T(8,128)(2,1)S(1)} %broadcast_select_fusion.3), channel_id=1, replica_groups=mesh['dp'=4,'ep'=8] {'ep'}, dimensions={0} | all-to-all | bytes 10485760 | tf_op jit(solution)/shard_map/all_to_all | solution.py:28
  262.5 9.0 reshape.448
  271.5 10.7 fusion.38
  282.2 17.9 %multiply_convert_fusion.5 = (bf16[2,4096,512]{1,2,0:T(8,128)(2,1)}, f32[2,4096,512]{1,2,0:T(8,128)}) fusion(f32[2,4096,512]{1,2,0:T(8,128)} %fusion.38, bf16[2,4096,320]{1,2,0:T(8,128)(2,1)} %reshape.448, bf16[2,320,512]{2,1,0:T(8,128)(2,1)S(1)} %copy-done.40), kind=kOutput, calls=%fused_computation.24 | convolution fusion | flops 2709520384 | bytes 47841280 | tf_op jit(solution)/shard_map/erd,edf->erf/dot_general | solution.py:49
  308.1 16.1 copy.137
  335.1 29.0 %scatter_custom_fusion.1 = s32[16]{0:T(128)S(1)} fusion(s32[4096]{0:T(1024)S(1)} %bitcast.215, s32[4096]{0:T(1024)S(1)} %broadcast.330, s32[]{:T(128)} %constant.53.clone.1), kind=kCustom, calls=%fused_computation.120 | custom fusion | flops 4096 | bytes 68 | tf_op jit(solution)/shard_map/scatter-add | solution.py:15
  373.6 45.5 %gather_fusion.3 = s32[8192]{0:T(1024)S(1)} fusion(s32[4096]{0:T(1024)S(1)} %get-tuple-element.16, s32[8192]{0:T(1024)S(1)} %broadcast_clamp_fusion), kind=kCustom, calls=%fused_computation.3 | custom fusion | bytes 98304 | tf_op jit(solution)/shard_map/gather | solution.py:19
  419.2 34.7 %gather_fusion.7 = bf16[8192,320]{1,0:T(8,128)(2,1)} fusion(bf16[4096,320]{1,0:T(8,128)(2,1)} %copy.148, s32[8192]{0:T(1024)S(1)} %broadcast_clamp_fusion.1), kind=kCustom, calls=%fused_computation.7 | custom fusion | bytes 10518528 | tf_op jit(solution)/shard_map/gather | solution.py:90
  492.4 20.3 %gather_fusion.2 = bf16[4096,320]{1,0:T(8,128)(2,1)} fusion(bf16[8192,320]{1,0:T(8,128)(2,1)} %bitcast.196, s32[4096]{0:T(1024)S(1)} %fusion.22), kind=kCustom, calls=%fused_computation.2 | custom fusion | bytes 5259264 | tf_op jit(solution)/shard_map/gather | solution.py:80
  517.6 11.5 fusion.13
  533.7 34.7 %gather_fusion.4 = bf16[8192,320]{1,0:T(8,128)(2,1)} fusion(bf16[4096,320]{1,0:T(8,128)(2,1)} %copy.141, s32[8192]{0:T(1024)S(1)} %broadcast_clamp_fusion.1), kind=kCustom, calls=%fused_computation.4 | custom fusion | bytes 10518528 | tf_op jit(solution)/shard_map/gather | solution.py:68
  585.3 121.3 %all_to_all.186 = bf16[8,2,512,320]{2,3,1,0:T(8,128)(2,1)} all-to-all(bf16[8,2,512,320]{2,3,1,0:T(8,128)(2,1)} %get-tuple-element.47), channel_id=1, replica_groups=mesh['dp'=4,'ep'=8] {'ep'}, dimensions={0} | all-to-all | bytes 10485760 | tf_op jit(solution)/shard_map/all_to_all | solution.py:28
  711.4 45.5 %gather_fusion.6 = f32[8192]{0:T(1024)S(1)} fusion(f32[4096]{0:T(1024)S(1)} %bitcast.190, s32[8192]{0:T(1024)S(1)} %broadcast_clamp_fusion.1), kind=kCustom, calls=%fused_computation.6 | custom fusion | bytes 98304 | tf_op jit(solution)/shard_map/gather | solution.py:91
  765.5 9.0 reshape.455
  774.4 10.6 fusion.42
  785.1 42.4 %all-to-all-done.5 = bf16[8,2,512,320]{2,3,1,0:T(8,128)(2,1)} async-done(((bf16[8,2,512,320]{2,3,1,0:T(8,128)(2,1)}), bf16[8,2,512,320]{2,3,1,0:T(8,128)(2,1)}, u32[]{:S(2)}, u32[]{:S(2)}) %all-to-all-start.5) | async-done | bytes 5242912 | tf_op jit(solution)/shard_map/all_to_all | solution.py:28
  831.1 10.6 fusion.41
  849.4 9.0 reshape.458
  858.3 26.0 %multiply_reduce_fusion = (f32[2,4096]{1,0:T(2,128)S(1)}, bf16[2,4096,512]{1,2,0:T(8,128)(2,1)}, bf16[2,4096,512]{1,2,0:T(8,128)(2,1)}, bf16[2,4096,512]{1,2,0:T(8,128)(2,1)}) fusion(f32[2,4096,512]{1,2,0:T(8,128)} %fusion.42, f32[2,4096,512]{1,2,0:T(8,128)} %fusion.41, f32[2,4096]{1,0:T(2,128)S(1)} %bitcast.230, bf16[2,4096,320]{1,2,0:T(8,128)(2,1)} %reshape.458, ...), kind=kOutput, calls=%fused_computation.16 | convolution fusion | flops 2768232448 | bytes 64684032 | tf_op jit(solution)/shard_map/erd,efd->erf/dot_general | solution.py:93
  898.0 16.2 copy.153
  919.5 45.9 %gather_fusion.9 = f32[8192]{0:T(1024)S(1)} fusion(f32[4096]{0:T(1024)S(1)} %bitcast.189, s32[8192]{0:T(1024)S(1)} %copy-done.19), kind=kCustom, calls=%fused_computation.9 | custom fusion | bytes 98304 | tf_op jit(solution)/shard_map/gather | solution.py:91
  995.7 12.6 fusion.18
  1012.4 20.4 %reduce.40 = f32[4096,2]{1,0:T(8,128)} reduce(f32[4096,1,2]{2,1,0:T(1,128)} %bitcast.208, f32[]{:T(128)} %broadcast.555), dimensions={1}, to_apply=%bitcast.134.reduce_sub_computation | reduce | bytes 65540
  1036.5 21.6 %all-to-all-done.6 = bf16[1,2,4096,320]{3,1,0,2:T(2,128)(2,1)} async-done(((bf16[1,2,4096,320]{3,1,0,2:T(2,128)(2,1)}), bf16[1,2,4096,320]{3,1,0,2:T(2,128)(2,1)}, u32[]{:S(2)}, u32[]{:S(2)}) %all-to-all-start.6) | async-done | bytes 5242912 | tf_op jit(solution)/shard_map/all_to_all | solution.py:36
  1068.0 20.3 %gather_fusion.8 = bf16[4096,320]{1,0:T(8,128)(2,1)} fusion(bf16[8192,320]{1,0:T(8,128)(2,1)} %bitcast.197, s32[4096]{0:T(1024)S(1)} %fusion.23), kind=kCustom, calls=%fused_computation.8 | custom fusion | bytes 5259264 | tf_op jit(solution)/shard_map/gather | solution.py:105
  1092.7 13.1 fusion.11
  1110.4 34.7 %gather_fusion.10 = bf16[8192,320]{1,0:T(8,128)(2,1)} fusion(bf16[4096,320]{1,0:T(8,128)(2,1)} %copy.156, s32[8192]{0:T(1024)S(1)} %copy-done.19), kind=kCustom, calls=%fused_computation.10 | custom fusion | bytes 10518528 | tf_op jit(solution)/shard_map/gather | solution.py:90
  1176.5 16.1 copy.145
  1192.6 92.2 %all-to-all-done.8 = bf16[8,2,512,320]{2,3,1,0:T(8,128)(2,1)} async-done(((bf16[8,2,512,320]{2,3,1,0:T(8,128)(2,1)}), bf16[8,2,512,320]{2,3,1,0:T(8,128)(2,1)}, u32[]{:S(2)}, u32[]{:S(2)}) %all-to-all-start.8) | async-done | bytes 5242912 | tf_op jit(solution)/shard_map/all_to_all | solution.py:28
  1289.7 8.9 fusion.47
  1306.4 9.0 reshape.461
  1315.3 24.5 %multiply_convert_fusion = (bf16[2,4096,512]{1,2,0:T(8,128)(2,1)}, bf16[2,4096,512]{1,2,0:T(8,128)(2,1)}, f32[2,4096]{1,0:T(2,128)S(1)}) fusion(f32[2,4096,512]{1,2,0:T(8,128)} %fusion.38, f32[2,4096]{1,0:T(2,128)S(1)} %bitcast.232, f32[2,4096,512]{1,2,0:T(8,128)} %get-tuple-element.82, bf16[2,4096,512]{1,2,0:T(8,128)(2,1)} %get-tuple-element.81, ...), kind=kOutput, calls=%fused_computation.18 | convolution fusion | flops 2755649536 | bytes 64684032 | tf_op jit(solution)/shard_map/erd,efd->erf/dot_general | solution.py:93
  1342.2 19.8 %reduce.38 = f32[4096,2]{1,0:T(8,128)} reduce(f32[4096,1,2]{2,1,0:T(1,128)S(1)} %bitcast.209, f32[]{:T(128)} %broadcast.555), dimensions={1}, to_apply=%bitcast.132.reduce_sub_computation | reduce | bytes 65540
  1365.7 9.0 fusion.50
  1374.7 53.6 %all-to-all-done.3 = bf16[1,2,4096,320]{3,1,0,2:T(2,128)(2,1)} async-done(((bf16[1,2,4096,320]{3,1,0,2:T(2,128)(2,1)}), bf16[1,2,4096,320]{3,1,0,2:T(2,128)(2,1)}, u32[]{:S(2)}, u32[]{:S(2)}) %all-to-all-start.3) | async-done | bytes 5242912 | tf_op jit(solution)/shard_map/all_to_all | solution.py:36
  1431.7 9.6 fusion.3
  1441.2 16.2 copy.161
  1462.7 8.9 fusion.48
  1485.3 40.6 %gather_fusion.13 = f32[4096]{0:T(1024)} fusion(f32[8192]{0:T(1024)S(1)} %bitcast.192, s32[4096]{0:T(1024)S(1)} %fusion.23), kind=kCustom, calls=%fused_computation.13 | custom fusion | bytes 49152 | tf_op jit(solution)/shard_map/gather | solution.py:106
  1532.4 20.3 %gather_fusion.5 = bf16[4096,320]{1,0:T(8,128)(2,1)} fusion(bf16[8192,320]{1,0:T(8,128)(2,1)} %bitcast.194, s32[4096]{0:T(1024)S(1)} %fusion.23), kind=kCustom, calls=%fused_computation.5 | custom fusion | bytes 5259264 | tf_op jit(solution)/shard_map/gather | solution.py:80
  1564.4 11.7 fusion.12
  1576.2 12.0 fusion.19
  1620.3 40.6 %gather_fusion.12 = f32[4096]{0:T(1024)} fusion(f32[8192]{0:T(1024)S(1)} %bitcast.193, s32[4096]{0:T(1024)S(1)} %copy-done.26), kind=kCustom, calls=%fused_computation.12 | custom fusion | bytes 49152 | tf_op jit(solution)/shard_map/gather | solution.py:106
  1667.3 20.3 %gather_fusion.11 = bf16[4096,320]{1,0:T(8,128)(2,1)} fusion(bf16[8192,320]{1,0:T(8,128)(2,1)} %bitcast.195, s32[4096]{0:T(1024)S(1)} %copy-done.26), kind=kCustom, calls=%fused_computation.11 | custom fusion | bytes 5259264 | tf_op jit(solution)/shard_map/gather | solution.py:105
  1692.5 13.0 fusion.10
  (203 shorter events, 355.8 us)
Async XLA Ops:
  0.6 857.7 %copy-start = (bf16[2,512,320]{1,2,0:T(8,128)(2,1)S(1)}, bf16[2,512,320]{1,2,0:T(8,128)(2,1)}, u32[]{:S(2)}) copy-start(bf16[2,512,320]{1,2,0:T(8,128)(2,1)} %param.32) | copy-start | bytes 1966084
  40.9 88.9 %copy-start.34 = (s32[8,2]{1,0:T(8,128)}, s32[8,2]{1,0:T(8,128)S(1)}, u32[]{:S(2)}) copy-start(s32[8,2]{1,0:T(8,128)S(1)} %lt.112) | copy-start | bytes 196
  86.8 34.7 %copy-start.18 = (s32[8192]{0:T(1024)}, s32[8192]{0:T(1024)S(1)}, u32[]{:S(2)}) copy-start(s32[8192]{0:T(1024)S(1)} %broadcast_clamp_fusion.3) | copy-start | bytes 98308
  129.9 127.3 %copy-start.29 = (pred[8,2,512]{2,1,0:T(4,128)(4,1)}, pred[8,2,512]{2,1,0:T(4,128)(4,1)S(1)}, u32[]{:S(2)}) copy-start(pred[8,2,512]{2,1,0:T(4,128)(4,1)S(1)} %iota_compare_fusion.1) | copy-start | bytes 24580
  262.5 9.0 copy-start.15
  271.5 10.7 copy-start.40
  282.2 17.9 %copy-start.38 = (bf16[2,512,320]{1,2,0:T(8,128)(2,1)S(1)}, bf16[2,512,320]{1,2,0:T(8,128)(2,1)}, u32[]{:S(2)}) copy-start(bf16[2,512,320]{1,2,0:T(8,128)(2,1)} %param.26) | copy-start | bytes 1966084
  324.2 10.8 copy-start.32
  324.2 46.6 %copy-start.9 = (bf16[4096,320]{0,1:T(8,128)(2,1)S(1)}, bf16[4096,320]{0,1:T(8,128)(2,1)}, u32[]{:S(2)}) copy-start(bf16[4096,320]{0,1:T(8,128)(2,1)} %param.19) | copy-start | bytes 7864324
  324.2 161.7 %all-to-all-start.1 = ((bf16[1,2,4096,320]{3,1,0,2:T(2,128)(2,1)}), bf16[1,2,4096,320]{3,1,0,2:T(2,128)(2,1)}, u32[]{:S(2)}, u32[]{:S(2)}) async-start(bf16[1,2,4096,320]{3,1,0,2:T(2,128)(2,1)} %copy.137), calls=%async_computation.1 | async-start | bytes 12582912 | tf_op jit(solution)/shard_map/all_to_all | solution.py:36
  369.8 49.3 %copy-start.1 = (s32[4096]{0:T(1024)}, s32[4096]{0:T(1024)S(1)}, u32[]{:S(2)}) copy-start(s32[4096]{0:T(1024)S(1)} %get-tuple-element.16) | copy-start | bytes 49156
  453.9 9.0 copy-start.31
  454.0 19.6 %copy-start.6 = (bf16[4096,320]{0,1:T(8,128)(2,1)S(1)}, bf16[4096,320]{0,1:T(8,128)(2,1)}, u32[]{:S(2)}) copy-start(bf16[4096,320]{0,1:T(8,128)(2,1)} %param.18) | copy-start | bytes 7864324
  473.6 18.8 %copy-start.25 = (s32[4096]{0:T(1024)}, s32[4096]{0:T(1024)S(1)}, u32[]{:S(2)}) copy-start(s32[4096]{0:T(1024)S(1)} %fusion.22) | copy-start | bytes 49156
  492.4 25.2 %copy-start.3 = (f32[4096,1]{0,1:T(1,128)S(1)}, f32[4096,1]{0,1:T(1,128)}, u32[]{:S(2)}) copy-start(f32[4096,1]{0,1:T(1,128)} %param.21) | copy-start | bytes 49156
  706.6 121.0 %all-to-all-start.5 = ((bf16[8,2,512,320]{2,3,1,0:T(8,128)(2,1)}), bf16[8,2,512,320]{2,3,1,0:T(8,128)(2,1)}, u32[]{:S(2)}, u32[]{:S(2)}) async-start(bf16[8,2,512,320]{2,3,1,0:T(8,128)(2,1)} %get-tuple-element.48), calls=%async_computation.5 | async-start | bytes 10485760 | tf_op jit(solution)/shard_map/all_to_all | solution.py:28
  765.5 9.0 copy-start.17
  774.4 56.6 %copy-start.14 = (bf16[2,320,512]{2,1,0:T(8,128)(2,1)S(1)}, bf16[2,320,512]{2,1,0:T(8,128)(2,1)}, u32[]{:S(2)}) copy-start(bf16[2,320,512]{2,1,0:T(8,128)(2,1)} %param.30) | copy-start | bytes 1966084
  827.5 30.8 %all-to-all-start.4 = ((f32[8,2,512]{2,1,0:T(2,128)}), f32[8,2,512]{2,1,0:T(2,128)S(1)}, u32[]{:S(2)}, u32[]{:S(2)}) async-start(f32[8,2,512]{2,1,0:T(2,128)} %broadcast_select_fusion.5), calls=%async_computation.4 | async-start | bytes 65536 | tf_op jit(solution)/shard_map/all_to_all | solution.py:28
  858.3 26.0 %copy-start.36 = (f32[8,2,512]{2,1,0:T(2,128)}, f32[8,2,512]{2,1,0:T(2,128)S(1)}, u32[]{:S(2)}) copy-start(f32[8,2,512]{2,1,0:T(2,128)S(1)} %all-to-all-done.4) | copy-start | bytes 98308
  914.2 143.9 %all-to-all-start.6 = ((bf16[1,2,4096,320]{3,1,0,2:T(2,128)(2,1)}), bf16[1,2,4096,320]{3,1,0,2:T(2,128)(2,1)}, u32[]{:S(2)}, u32[]{:S(2)}) async-start(bf16[1,2,4096,320]{3,1,0,2:T(2,128)(2,1)} %copy.153), calls=%async_computation.6 | async-start | bytes 12582912 | tf_op jit(solution)/shard_map/all_to_all | solution.py:36
  919.4 46.0 %copy-start.2 = (s32[4096]{0:T(1024)S(1)}, s32[4096]{0:T(1024)}, u32[]{:S(2)}) copy-start(s32[4096]{0:T(1024)} %copy-done.1) | copy-start | bytes 49156
  919.4 51.8 %copy-start.28 = (s32[16]{0:T(128)S(1)}, s32[16]{0:T(128)}, u32[]{:S(2)}) copy-start(s32[16]{0:T(128)} %copy-done.27) | copy-start | bytes 196
  919.4 52.5 %copy-start.33 = (s32[4096,1]{0,1:T(1,128)S(1)}, s32[4096,1]{0,1:T(1,128)}, u32[]{:S(2)}) copy-start(s32[4096,1]{0,1:T(1,128)} %param.22) | copy-start | bytes 49156
  919.4 57.4 %copy-start.35 = (s32[8,2]{1,0:T(8,128)S(1)}, s32[8,2]{1,0:T(8,128)}, u32[]{:S(2)}) copy-start(s32[8,2]{1,0:T(8,128)} %copy-done.34) | copy-start | bytes 196
  919.4 63.9 %copy-start.10 = (bf16[4096,320]{0,1:T(8,128)(2,1)S(1)}, bf16[4096,320]{0,1:T(8,128)(2,1)}, u32[]{:S(2)}) copy-start(bf16[4096,320]{0,1:T(8,128)(2,1)} %param.19) | copy-start | bytes 7864324
  983.4 6.7 copy-start.7
  995.7 12.6 copy-start.13
  1058.1 95.1 %all-to-all-start.7 = ((f32[8,2,512]{2,1,0:T(2,128)}), f32[8,2,512]{2,1,0:T(2,128)S(1)}, u32[]{:S(2)}, u32[]{:S(2)}) async-start(f32[8,2,512]{2,1,0:T(2,128)} %broadcast_select_fusion.4), calls=%async_computation.7 | async-start | bytes 65536 | tf_op jit(solution)/shard_map/all_to_all | solution.py:28
  1145.1 13.2 copy-start.30
  1153.2 10.6 all-to-all-start.11
  1163.8 121.0 %all-to-all-start.8 = ((bf16[8,2,512,320]{2,3,1,0:T(8,128)(2,1)}), bf16[8,2,512,320]{2,3,1,0:T(8,128)(2,1)}, u32[]{:S(2)}, u32[]{:S(2)}) async-start(bf16[8,2,512,320]{2,3,1,0:T(8,128)(2,1)} %broadcast_select_fusion.2), calls=%async_computation.8 | async-start | bytes 10485760 | tf_op jit(solution)/shard_map/all_to_all | solution.py:28
  1284.7 143.6 %all-to-all-start.3 = ((bf16[1,2,4096,320]{3,1,0,2:T(2,128)(2,1)}), bf16[1,2,4096,320]{3,1,0,2:T(2,128)(2,1)}, u32[]{:S(2)}, u32[]{:S(2)}) async-start(bf16[1,2,4096,320]{3,1,0,2:T(2,128)(2,1)} %copy.145), calls=%async_computation.3 | async-start | bytes 12582912 | tf_op jit(solution)/shard_map/all_to_all | solution.py:36
  1306.4 9.0 copy-start.39
  1339.8 25.9 %copy-start.16 = (bf16[2,320,512]{2,1,0:T(8,128)(2,1)S(1)}, bf16[2,320,512]{2,1,0:T(8,128)(2,1)}, u32[]{:S(2)}) copy-start(bf16[2,320,512]{2,1,0:T(8,128)(2,1)} %param.24) | copy-start | bytes 1966084
  1365.7 66.0 %copy-start.41 = (bf16[2,320,512]{2,1,0:T(8,128)(2,1)S(1)}, bf16[2,320,512]{2,1,0:T(8,128)(2,1)}, u32[]{:S(2)}) copy-start(bf16[2,320,512]{2,1,0:T(8,128)(2,1)} %param.25) | copy-start | bytes 1966084
  1428.3 29.2 %all-to-all-start.10 = ((f32[8,1,1024]{2,1,0:T(1,128)}), f32[8,1,1024]{2,1,0:T(1,128)S(1)}, u32[]{:S(2)}, u32[]{:S(2)}) async-start(f32[8,1,1024]{2,1,0:T(1,128)} %reshape.768), calls=%async_computation.10 | async-start | bytes 65536 | tf_op jit(solution)/shard_map/all_to_all | solution.py:36
  1457.5 203.4 %all-to-all-start.9 = ((bf16[1,2,4096,320]{3,1,0,2:T(2,128)(2,1)}), bf16[1,2,4096,320]{3,1,0,2:T(2,128)(2,1)}, u32[]{:S(2)}, u32[]{:S(2)}) async-start(bf16[1,2,4096,320]{3,1,0,2:T(2,128)(2,1)} %copy.161), calls=%async_computation.9 | async-start | bytes 12582912 | tf_op jit(solution)/shard_map/all_to_all | solution.py:36
  1462.7 8.9 copy-start.37
  1557.6 6.8 copy-start.5
  1557.6 6.8 copy-start.8
  1557.6 6.8 copy-start.22
  1557.6 18.5 %slice-start.2 = ((s8[8388608]{0:T(1024)(128)(4,1)}), s8[4194304]{0:T(1024)(128)(4,1)S(1)}, s32[]{:S(2)}) async-start(s8[8388608]{0:T(1024)(128)(4,1)} %bitcast.206), calls=%async_computation.14 | async-start | bytes 8388608
  1564.4 11.8 slice-start.3
  1564.4 11.7 copy-start.24
  1564.4 23.8 %slice-start = ((s8[5242880]{0:T(1024)(128)(4,1)}), s8[4194304]{0:T(1024)(128)(4,1)S(1)}, s32[]{:S(2)}) async-start(s8[5242880]{0:T(1024)(128)(4,1)} %bitcast.204), calls=%async_computation.12 | async-start | bytes 8388608
  1576.1 12.0 slice-start.1
  1603.7 16.6 copy-start.26
  (8 other events, 34.4 us)
where the time goes:
time: 1720 us; the launch traced here: 1710 us
  local copies, waits for them, and re-layouts  736 us (43%)
  matrix products  304 us (18%)
  blocking collectives  246 us (14%)
  waiting for transfers between devices  210 us (12%)
  other arithmetic  163 us (9%)
  starting transfers between devices  45.2 us (3%)
    all_to_all x2, blocking collectives, to_experts(): received = lax.all_to_all(shaped, 'ep', 0, 2, tiled=True)  246 us
    all_to_all x4, waiting for transfers between devices, to_experts(): received = lax.all_to_all(shaped, 'ep', 0, 2, tiled=True)  135 us
    gather x4, local copies, waits for them, and re-layouts, layer_backward(): gates.reshape(-1)[src_pair]  91.5 us
    gather x2, local copies, waits for them, and re-layouts, route_tables(): pair_order[jnp.minimum(expert_start[:, None] + slot_index[None, :], pair_...  91.1 us
    gather x4, local copies, waits for them, and re-layouts, layer_backward(): d_next[src_pair // top_k]  85.9 us
    gather x4, local copies, waits for them, and re-layouts, send_rows(): sent = jnp.where(tables[1][:, None], rows[tables[0] // top_k], 0)  85.8 us
    gather x2, local copies, waits for them, and re-layouts, layer_backward(): d_gates = gate_back[position].reshape(tokens, top_k)  81.1 us
    all_to_all x6, waiting for transfers between devices, to_sources(): received = lax.all_to_all(shaped, 'ep', 2, 0, tiled=True)  75.6 us
  transfers between devices with their start and end apart: 10, of which 5 were waited for; matrix products, arithmetic and copies ran while one was open for 47% of the time, Pallas kernels for 0%

commit v1 on v0

v1 whole, which is shorter than its diff:
```python
import functools

import jax
import jax.numpy as jnp
from jax import lax
from jax.experimental import pallas as pl
from jax.experimental.pallas import tpu as pltpu
from jax.sharding import PartitionSpec as P

TILE = 256
LANES = 384
F32 = jnp.float32
BF16 = jnp.bfloat16


def slot_capacity(tokens, n_experts, top_k):
    return top_k * ((2 * tokens + n_experts - 1) // n_experts)


def mm(a, b):
    return jnp.dot(a, b, preferred_element_type=F32)


def mm_nt(a, b):
    return lax.dot_general(a, b, (((1,), (1,)), ((), ())), preferred_element_type=F32)


def mm_tn(a, b):
    return lax.dot_general(a, b, (((0,), (0,)), ((), ())), preferred_element_type=F32)


def row_to_column(row):
    return jnp.transpose(jnp.broadcast_to(row, (128, row.shape[1])))[:, :1]


def cost(flops, nbytes):
    return pl.CostEstimate(flops=int(flops), bytes_accessed=int(nbytes), transcendentals=0)


def tables_body(idx_ref, pos_ref, cnt_ref, *, n_experts, capacity):
    chunks = idx_ref.shape[1]
    earlier = (lax.broadcasted_iota(jnp.int32, (TILE, TILE), 0)
               < lax.broadcasted_iota(jnp.int32, (TILE, TILE), 1)).astype(F32).astype(BF16)
    expert = lax.broadcasted_iota(jnp.int32, (n_experts, TILE), 0)
    base = (lax.broadcasted_iota(jnp.int32, (n_experts, TILE), 0) * capacity).astype(F32)
    for layer in range(2):
        carry = jnp.zeros((n_experts, 1), F32)
        for c in range(chunks):
            hot = (expert == idx_ref[layer, c:c + 1, :]).astype(F32)
            before = mm(hot.astype(BF16), earlier)
            where = jnp.sum(hot * (before + carry + base), axis=0, keepdims=True)
            pos_ref[layer, c:c + 1, :] = where.astype(jnp.int32)
            carry = carry + jnp.sum(hot, axis=1, keepdims=True)
        cnt_ref[layer] = jnp.broadcast_to(carry, (n_experts, 128)).astype(jnp.int32)


def route_tables(idx_a, idx_b, n_experts, capacity):
    chunks = idx_a.size // TILE
    idx = jnp.stack([idx_a.reshape(chunks, TILE), idx_b.reshape(chunks, TILE)])
    pos, cnt = pl.pallas_call(
        functools.partial(tables_body, n_experts=n_experts, capacity=capacity),
        out_shape=(jax.ShapeDtypeStruct((2, chunks, TILE), jnp.int32),
                   jax.ShapeDtypeStruct((2, n_experts, 128), jnp.int32)),
        name="tables", cost_estimate=cost(3e8, 1e5))(idx)
    return pos.reshape(2, -1), cnt[:, :, 0]


def sort_body(pos_ref, x_ref, *refs, with_gate):
    if with_gate:
        gate_ref, out_ref, gout_ref, wide, slots = refs
    else:
        out_ref, wide, slots = refs
    tokens, width = x_ref.shape
    n_slots = out_ref.shape[0]

    @pl.loop(0, n_slots // TILE)
    def _(c):
        slots[pl.ds(c * TILE, TILE), :] = jnp.zeros((TILE, LANES), F32)

    @pl.loop(0, tokens // TILE)
    def _(c):
        at = pl.ds(c * TILE, TILE)
        wide[at, :width] = x_ref[at, :].astype(F32)
        if with_gate:
            wide[at, width:] = jnp.broadcast_to(row_to_column(gate_ref[pl.ds(c, 1), :]), (TILE, LANES - width))

    unroll = 32

    @pl.loop(0, tokens // unroll)
    def _(c):
        rows = [wide[pl.ds(c * unroll + i, 1), :] for i in range(unroll)]
        for i in range(unroll):
            slots[pl.ds(pos_ref[c * unroll + i], 1), :] = rows[i]

    @pl.loop(0, n_slots // TILE)
    def _(c):
        at = pl.ds(c * TILE, TILE)
        out_ref[at, :] = slots[at, :width].astype(BF16)
        if with_gate:
            gout_ref[pl.ds(c, 1), :] = jnp.transpose(slots[at, LANES - 128:])[127:128, :]


def sort_rows(pos, x, n_slots, gate=None):
    tokens, width = x.shape
    with_gate = gate is not None
    out_shape = [jax.ShapeDtypeStruct((n_slots, width), BF16)]
    args = [pos, x]
    if with_gate:
        args.append(gate)
        out_shape.append(jax.ShapeDtypeStruct((n_slots // TILE, TILE), F32))
    vmem = pl.BlockSpec(memory_space=pltpu.VMEM)
    return pl.pallas_call(
        functools.partial(sort_body, with_gate=with_gate),
        out_shape=out_shape,
        in_specs=[pl.BlockSpec(memory_space=pltpu.SMEM)] + [vmem] * (len(args) - 1),
        out_specs=[vmem] * len(out_shape),
        scratch_shapes=[pltpu.VMEM((tokens, LANES), F32), pltpu.VMEM((n_slots, LANES), F32)],
        name="sort_rows", cost_estimate=cost(2e9, 9e6))(*args)


def gather_rows(pos_ref, start, table, out):
    unroll = 16

    @pl.loop(0, TILE // unroll)
    def _(c):
        where = [pos_ref[start + c * unroll + i] for i in range(unroll)]
        rows = [table[pl.ds(p, 1), :] for p in where]
        for i in range(unroll):
            out[pl.ds(c * unroll + i, 1), :] = rows[i]


def expert_weights(w_ref):
    depth = w_ref.shape[0] * w_ref.shape[3]
    return tuple(w_ref[:, 0, m].reshape(depth, w_ref.shape[4]) for m in range(3))


def swiglu(a1, a3):
    sigma = jax.nn.sigmoid(a1)
    return sigma, (a1 * sigma * a3).astype(BF16)


def swiglu_grads(a1, a3, sigma, q):
    qs = q * sigma
    d1 = qs * a3 * (1.0 + a1 * (1.0 - sigma))
    return d1.astype(BF16), (qs * a1).astype(BF16)


def token_body(pos_ref, cnt_ref, *refs, fwd, bwd, n_experts, capacity):
    refs = list(refs)
    xs_ref = refs.pop(0)
    if bwd:
        dys_ref, gs_ref = refs.pop(0), refs.pop(0)
    w_ref, x_ref = refs.pop(0), refs.pop(0)
    if bwd:
        dy_ref = refs.pop(0)
    if fwd:
        g_ref = refs.pop(0)
    s1_ref, s3_ref, s2_ref = refs.pop(0), refs.pop(0), refs.pop(0)
    if fwd:
        y_ref = refs.pop(0)
    if bwd:
        dx_ref, dg_ref = refs.pop(0), refs.pop(0)
    if fwd:
        o_all, o_tmp = refs.pop(0), refs.pop(0)
    if bwd:
        du_all, du_tmp = refs.pop(0), refs.pop(0)
    step = pl.program_id(0)
    width = x_ref.shape[1]
    per = capacity // TILE

    for t in range(per):
        @pl.when(jnp.logical_and(step < n_experts, cnt_ref[jnp.minimum(step, n_experts - 1)] > t * TILE))
        def _():
            w1, w3, w2t = expert_weights(w_ref)
            rows = slice(t * TILE, (t + 1) * TILE)
            at = pl.ds(pl.multiple_of(step * capacity + t * TILE, TILE), TILE)
            u = xs_ref[0, rows, :]
            a1, a3 = mm(u, w1), mm(u, w3)
            sigma, h = swiglu(a1, a3)
            if fwd:
                o_all[at, :width] = mm_nt(h, w2t).astype(BF16).astype(F32)
            if bwd:
                p = mm(dys_ref[0, rows, :], w2t)
                dgate = jnp.sum(h.astype(F32) * p, axis=1, keepdims=True)
                g = row_to_column(gs_ref[pl.ds(step * per + t, 1), :])
                d1, d3 = swiglu_grads(a1, a3, sigma, g * p)
                du_all[at, :width] = (mm_nt(d1, w1) + mm_nt(d3, w3)).astype(BF16).astype(F32)
                du_all[at, width:] = jnp.broadcast_to(dgate, (TILE, LANES - width))

    @pl.when(step >= n_experts)
    def _():
        tile = step - n_experts
        start = tile * TILE
        if fwd:
            gather_rows(pos_ref, start, o_all, o_tmp)
        if bwd:
            gather_rows(pos_ref, start, du_all, du_tmp)
        x = x_ref[...]
        a1, a3 = mm(x, s1_ref[...]), mm(x, s3_ref[...])
        sigma, h = swiglu(a1, a3)
        if fwd:
            shared = mm(h, s2_ref[...])
            g = row_to_column(g_ref[pl.ds(tile, 1), :])
            y_ref[...] = (x.astype(F32) + shared + g * o_tmp[:, :width]).astype(BF16)
        if bwd:
            dy = dy_ref[...]
            p = mm_nt(dy, s2_ref[...])
            d1, d3 = swiglu_grads(a1, a3, sigma, p)
            dxs = mm_nt(d1, s1_ref[...]) + mm_nt(d3, s3_ref[...])
            dx_ref[...] = (dy.astype(F32) + dxs + du_tmp[:, :width]).astype(BF16)
            dg_ref[pl.ds(tile, 1), :] = jnp.transpose(du_tmp[:, LANES - 128:])[127:128, :]


def token_layer(pos, cnt, xs, weights, x, shared, capacity, gate=None, dys=None, gs=None, dy=None):
    fwd, bwd = gate is not None, dys is not None
    tokens, width = x.shape
    n_experts = cnt.shape[0]
    s1, s3, s2 = shared
    last = n_experts - 1
    expert_map = lambda i, *_: (jnp.minimum(i, last), 0, 0)
    token_map = lambda i, *_: (jnp.maximum(i - n_experts, 0), 0)
    whole = lambda a: pl.BlockSpec(a.shape, lambda i, *_: (0,) * a.ndim)
    rows = pl.BlockSpec((1, capacity, width), expert_map)
    toks = pl.BlockSpec((TILE, width), token_map)
    q, _, m, qd, ff = weights.shape
    wspec = pl.BlockSpec((q, 1, m, qd, ff), lambda i, *_: (0, jnp.minimum(i, last), 0, 0, 0))
    args, specs, outs, ospecs, scratch = [], [], [], [], []

    def add(a, s):
        args.append(a)
        specs.append(s)

    add(xs.reshape(n_experts, capacity, width), rows)
    if bwd:
        add(dys.reshape(n_experts, capacity, width), rows)
        add(gs, whole(gs))
    add(weights, wspec)
    add(x, toks)
    if bwd:
        add(dy, toks)
    if fwd:
        add(gate, whole(gate))
    for s in (s1, s3, s2):
        add(s, whole(s))
    slots = n_experts * capacity
    if fwd:
        outs.append(jax.ShapeDtypeStruct((tokens, width), BF16))
        ospecs.append(toks)
        scratch += [pltpu.VMEM((slots, LANES), F32), pltpu.VMEM((TILE, LANES), F32)]
    if bwd:
        outs += [jax.ShapeDtypeStruct((tokens, width), BF16), jax.ShapeDtypeStruct((tokens // TILE, TILE), F32)]
        ospecs += [toks, pl.BlockSpec((tokens // TILE, TILE), lambda i, *_: (0, 0))]
        scratch += [pltpu.VMEM((slots, LANES), F32), pltpu.VMEM((TILE, LANES), F32)]
    n_mm = (3 if fwd else 2) + (3 if bwd else 0)
    return pl.pallas_call(
        functools.partial(token_body, fwd=fwd, bwd=bwd, n_experts=n_experts, capacity=capacity),
        out_shape=outs,
        grid_spec=pltpu.PrefetchScalarGridSpec(
            num_scalar_prefetch=2, grid=(n_experts + tokens // TILE,),
            in_specs=specs, out_specs=ospecs, scratch_shapes=scratch),
        name="token_layer",
        cost_estimate=cost(2 * n_mm * 2 * tokens * width * ff, 3e7))(pos, cnt, *args)


def wgrad_body(cnt_ref, x_ref, dy_ref, g_ref, w1_ref, w3_ref, w2_ref, dw1_ref, dw3_ref, dw2_ref):
    e, src = pl.program_id(0), pl.program_id(1)
    per = x_ref.shape[2] // TILE

    @pl.when(src == 0)
    def _():
        dw1_ref[...] = jnp.zeros_like(dw1_ref)
        dw3_ref[...] = jnp.zeros_like(dw3_ref)
        dw2_ref[...] = jnp.zeros_like(dw2_ref)

    for t in range(per):
        @pl.when(cnt_ref[src, e] > t * TILE)
        def _():
            rows = slice(t * TILE, (t + 1) * TILE)
            u, dy = x_ref[0, 0, rows, :], dy_ref[0, 0, rows, :]
            g = row_to_column(g_ref[src, pl.ds(e * per + t, 1), :])
            a1, a3 = mm(u, w1_ref[0]), mm(u, w3_ref[0])
            sigma, h = swiglu(a1, a3)
            p = mm_nt(dy, w2_ref[0])
            scaled = (g * dy.astype(F32)).astype(BF16)
            dw2_ref[0] += mm_tn(h, scaled)
            d1, d3 = swiglu_grads(a1, a3, sigma, g * p)
            dw1_ref[0] += mm_tn(u, d1)
            dw3_ref[0] += mm_tn(u, d3)


def weight_grads(x_rows, dy_rows, gates, w1, w3, w2, capacity):
    n_local, width, ff = w1.shape
    group = x_rows.shape[0]
    counts = jnp.sum(gates.reshape(group, n_local, capacity) > 0.0, axis=2, dtype=jnp.int32)
    shape = (group, n_local, capacity, width)
    rows = pl.BlockSpec((1, 1, capacity, width), lambda e, s, *_: (s, e, 0, 0))
    mat = lambda a: pl.BlockSpec((1,) + a.shape[1:], lambda e, s, *_: (e, 0, 0))
    grads = [jax.ShapeDtypeStruct(a.shape, F32) for a in (w1, w3, w2)]
    return pl.pallas_call(
        wgrad_body,
        out_shape=grads,
        grid_spec=pltpu.PrefetchScalarGridSpec(
            num_scalar_prefetch=1, grid=(n_local, group),
            in_specs=[rows, rows, pl.BlockSpec(gates.shape, lambda e, s, *_: (0, 0, 0)),
                      mat(w1), mat(w3), mat(w2)],
            out_specs=[mat(w1), mat(w3), mat(w2)]),
        name="weight_grads",
        cost_estimate=cost(6 * 2 * group * n_local * capacity * width * ff, 2e7),
    )(counts, x_rows.reshape(shape), dy_rows.reshape(shape), gates, w1, w3, w2)


def exchange(rows, group_size):
    shaped = rows.reshape((group_size, rows.shape[0] // group_size) + rows.shape[1:])
    return lax.all_to_all(shaped, 'ep', 0, 0, tiled=True)


def gather_weights(w1, w3, w2, replicas):
    quarter = w1.shape[1] // replicas
    at = lax.axis_index('dp') * quarter
    part = jnp.stack([lax.dynamic_slice_in_dim(w1, at, quarter, 1),
                      lax.dynamic_slice_in_dim(w3, at, quarter, 1),
                      jnp.swapaxes(lax.dynamic_slice_in_dim(w2, at, quarter, 2), 1, 2)], axis=1)
    whole = lax.all_gather(part, ('dp', 'ep'), axis=0, tiled=True)
    return whole.reshape((replicas, -1) + whole.shape[1:])


def solution(mesh):
    group_size = mesh.shape['ep']
    replicas = mesh.shape['dp']
    token_spec = P(('dp', 'ep'), None)
    expert_spec = P('ep', None, None)
    shared_spec = P(None, None)
    grad_spec = P(('dp', 'ep'), None, None)
    layer_specs = (expert_spec,) * 3 + (shared_spec,) * 3

    def device_step(x_in, d_out, idx_a, gate_a, idx_b, gate_b,
                    w1_a, w3_a, w2_a, ws1_a, ws3_a, ws2_a,
                    w1_b, w3_b, w2_b, ws1_b, ws3_b, ws2_b):
        shared_a, shared_b = (ws1_a, ws3_a, ws2_a), (ws1_b, ws3_b, ws2_b)
        tokens, top_k = idx_a.shape
        n_experts = w1_a.shape[0] * group_size
        capacity = slot_capacity(tokens, n_experts, top_k)
        n_slots = n_experts * capacity
        gate_a, gate_b = gate_a.reshape(-1, TILE), gate_b.reshape(-1, TILE)
        all_a = gather_weights(w1_a, w3_a, w2_a, replicas)
        pos, cnt = route_tables(idx_a, idx_b, n_experts, capacity)
        pos_a, pos_b, cnt_a, cnt_b = pos[0], pos[1], cnt[0], cnt[1]
        dys_b, gs_b = sort_rows(pos_b, d_out, n_slots, gate_b)
        dy_rows_b, g_rows_b = exchange(dys_b, group_size), exchange(gs_b, group_size)
        xs_a, = sort_rows(pos_a, x_in, n_slots)
        x_rows_a = exchange(xs_a, group_size)
        x_mid, = token_layer(pos_a, cnt_a, xs_a, all_a, x_in, shared_a, capacity, gate=gate_a)
        all_b = gather_weights(w1_b, w3_b, w2_b, replicas)
        xs_b, = sort_rows(pos_b, x_mid, n_slots)
        x_rows_b = exchange(xs_b, group_size)
        x_last, d_mid, dgate_b = token_layer(pos_b, cnt_b, xs_b, all_b, x_mid, shared_b, capacity,
                                             gate=gate_b, dys=dys_b, gs=gs_b, dy=d_out)
        w1_r, w3_r, w2_r, x_again, _ = lax.optimization_barrier((w1_a, w3_a, w2_a, x_in, x_mid))
        all_a2 = gather_weights(w1_r, w3_r, w2_r, replicas)
        dys_a, gs_a = sort_rows(pos_a, d_mid, n_slots, gate_a)
        dy_rows_a, g_rows_a = exchange(dys_a, group_size), exchange(gs_a, group_size)
        xs_a2, = sort_rows(pos_a, x_again, n_slots)
        d_first, dgate_a = token_layer(pos_a, cnt_a, xs_a2, all_a2, x_again, shared_a, capacity,
                                       dys=dys_a, gs=gs_a, dy=d_mid)
        dw1_b, dw3_b, dw2_b = weight_grads(x_rows_b, dy_rows_b, g_rows_b, w1_b, w3_b, w2_b, capacity)
        dw1_a, dw3_a, dw2_a = weight_grads(x_rows_a, dy_rows_a, g_rows_a, w1_a, w3_a, w2_a, capacity)
        return (x_last, d_first, dw1_a, dw3_a, dw2_a, dw1_b, dw3_b, dw2_b,
                dgate_a.reshape(tokens, top_k), dgate_b.reshape(tokens, top_k))

    in_specs = (token_spec,) * 6 + layer_specs + layer_specs
    out_specs = (token_spec, token_spec) + (grad_spec,) * 6 + (token_spec, token_spec)
    return jax.shard_map(device_step, mesh=mesh, in_specs=in_specs, out_specs=out_specs, check_vma=False)
```

time: 1720 us -> 887 us (0.52)
  local copies, waits for them, and re-layouts: 736 us -> 154 us
  Pallas kernels: 0 us -> 346 us
  matrix products: 304 us -> 0 us
  blocking collectives: 246 us -> 0 us
  other arithmetic: 163 us -> 4.98 us
  waiting for transfers between devices: 210 us -> 317 us
    gather x26 -> x0, local copies, waits for them, and re-layouts: 537 us -> none  [the longest x4 91.5 us: layer_backward(): gates.reshape(-1)[src_pair]]
    pallas_call x0 -> x11, Pallas kernels: none -> 346 us  [the longest x3 182 us: token_layer(): pl.pallas_call(functools.partial(token_body, fwd=fwd, bwd=bwd, n_experts=...]
    dot_general x30 -> x0, matrix products: 304 us -> none  [the longest x2 50.5 us: layer_backward(): jnp.einsum('erd,efd->erf', dy_rows, w_down, preferred_element_type=jnp.fl...]
    all_to_all x2 -> x0, blocking collectives: 246 us -> none  [to_experts(): received = lax.all_to_all(shaped, 'ep', 0, 2, tiled=True)]
    all_gather x0 -> x3, waiting for transfers between devices: none -> 128 us  [gather_weights(): whole = lax.all_gather(part, ('dp', 'ep'), axis=0, tiled=True)]
    reshape x10 -> x8, local copies, waits for them, and re-layouts: 106 us -> 36.6 us  [the longest x6 35.4 us: exchange(): rows.reshape((group_size, rows.shape[0] // group_size) + rows.shape[1:])]
    scatter-add x2 -> x0, other arithmetic: 57.9 us -> none  [route_tables(): jax.ops.segment_sum(jnp.ones_like(flat_ids), flat_ids, num_segments=n_exp...]
    all_gather x0 -> x3, local copies, waits for them, and re-layouts: none -> 39.8 us  [gather_weights(): whole = lax.all_gather(part, ('dp', 'ep'), axis=0, tiled=True)]
  transfers between devices with their start and end apart: 10 -> 9, of which waited for: 5 -> 5; matrix products, arithmetic and copies ran while one was open for 47% -> 16% of each run, Pallas kernels for 0% -> 33%
where the time goes in v1:
time: 887 us; the launch traced here: 880 us
  Pallas kernels  346 us (39%)
  waiting for transfers between devices  317 us (36%)
  local copies, waits for them, and re-layouts  154 us (17%)
  starting transfers between devices  45.3 us (5%)
  between operations  13.9 us (2%)
    all_to_all x6, waiting for transfers between devices, exchange(): return lax.all_to_all(shaped, 'ep', 0, 0, tiled=True)  189 us
    pallas_call x3, Pallas kernels, token_layer(): pl.pallas_call(functools.partial(token_body, fwd=fwd, bwd=bwd, n_experts=...  182 us
    all_gather x3, waiting for transfers between devices, gather_weights(): whole = lax.all_gather(part, ('dp', 'ep'), axis=0, tiled=True)  128 us
    pallas_call x5, Pallas kernels, sort_rows(): pl.pallas_call(functools.partial(sort_body, with_gate=with_gate), out_sha...  111 us
    pallas_call x2, Pallas kernels, weight_grads(): pl.pallas_call(wgrad_body, out_shape=grads, grid_spec=pltpu.PrefetchScala...  51.3 us
    all_to_all x6, starting transfers between devices, exchange(): return lax.all_to_all(shaped, 'ep', 0, 0, tiled=True)  45.2 us
    all_gather x3, local copies, waits for them, and re-layouts, gather_weights(): whole = lax.all_gather(part, ('dp', 'ep'), axis=0, tiled=True)  39.8 us
    reshape x6, local copies, waits for them, and re-layouts, exchange(): rows.reshape((group_size, rows.shape[0] // group_size) + rows.shape[1:])  35.4 us
  transfers between devices with their start and end apart: 9, of which 5 were waited for; matrix products, arithmetic and copies ran while one was open for 16% of the time, Pallas kernels for 33%

profile of v1, /device:TPU:0, one launch (start us, length us, event | category | flops | bytes accessed | tf_op | source)
XLA Modules:
  0.0 880.4 jit_solution(7260413635433467147)
XLA Ops:
  8.2 0.9 dynamic-slice_bitcast_fusion.7
  11.9 1.0 dynamic-slice_bitcast_fusion.4
  15.9 2.1 tables.1
  21.1 4.7 copy.68.x_ref.refs_5_
  25.8 25.1 %sort_rows.7 = (bf16[8192,320]{1,0:T(8,128)(2,1)}, f32[32,256]{1,0:T(8,128)}) custom-call(s32[4096]{0:T(1024)} %bitcast.89, bf16[4096,320]{1,0:T(8,128)(2,1)} %copy.68.x_ref.refs_5_, f32[16,256]{1,0:T(8,128)} %reshape.103.refs_0_.refs_6_), custom_call_target="tpu_custom_call" | custom-call | flops 2000000000 | bytes 9000000 | tf_op jit(solution)/shard_map/sort_rows/pallas_call | solution.py:112
  51.0 1.4 reshape.114
  52.3 6.4 all-to-all-start.3
  59.3 2.8 copy.64.x_ref.refs_2_
  62.1 20.2 %sort_rows.5 = bf16[8192,320]{1,0:T(8,128)(2,1)} custom-call(s32[4096]{0:T(1024)} %bitcast.84, bf16[4096,320]{1,0:T(8,128)(2,1)} %copy.64.x_ref.refs_2_), custom_call_target="tpu_custom_call" | custom-call | flops 2000000000 | bytes 9000000 | tf_op jit(solution)/shard_map/sort_rows/pallas_call | solution.py:112
  82.3 8.1 copy.77
  90.5 5.2 all-to-all-start.1
  98.7 43.5 %all-gather.4.cloned.1.call-done = bf16[64,3,80,512]{3,2,0,1:T(8,128)(2,1)} async-done(((bf16[2,3,80,512]{3,2,0,1:T(8,128)(2,1)}), bf16[64,3,80,512]{3,2,0,1:T(8,128)(2,1)}) %all-gather.4.cloned.1.call-update) | async-done | bytes 15728656 | tf_op jit(solution)/shard_map/all_gather | solution.py:323
  142.2 13.4 %copy.65 = bf16[64,3,80,512]{3,2,1,0:T(8,128)(2,1)} copy(bf16[64,3,80,512]{3,2,0,1:T(8,128)(2,1)} %all-gather.4.cloned.1.call-done) | data formatting | bytes 31457280 | tf_op jit(solution)/shard_map/all_gather | solution.py:323
  155.6 47.0 %token_layer.3.x_ref.refs_4_ = bf16[4096,320]{1,0:T(8,128)(2,1)} custom-call(s32[4096]{0:T(1024)} %bitcast.85, s32[16]{0:T(128)} %get-tuple-element.82.cnt_ref, bf16[16,512,320]{2,1,0:T(8,128)(2,1)} %bitcast.71, bf16[4,16,3,80,512]{4,3,2,1,0:T(8,128)(2,1)} %bitcast.74, bf16[4096,320]{1,0:T(8,128)(2,1)} %copy.64.x_ref.refs_2_, ...), custom_call_target="tpu_custom_call" | custom-call | flops 8053063680 | bytes 30000000 | tf_op jit(solution)/shard_map/token_layer/pallas_call | solution.py:255
  202.6 1.0 dynamic-slice_bitcast_fusion.1
  204.5 8.2 copy.86
  212.7 51.2 %all-to-all-done.1 = bf16[8,1024,320]{1,2,0:T(8,128)(2,1)} async-done(((bf16[8,1024,320]{1,2,0:T(8,128)(2,1)}), bf16[8,1024,320]{1,2,0:T(8,128)(2,1)}, u32[]{:S(2)}, u32[]{:S(2)}) %all-to-all-start.1) | async-done | bytes 5242912 | tf_op jit(solution)/shard_map/all_to_all | solution.py:314
  263.8 4.7 all-to-all-start.5
  268.5 1.9 copy.71.refs_9_
  270.4 84.0 %all-gather.6.cloned.1.call-done = bf16[64,3,80,512]{3,2,0,1:T(8,128)(2,1)} async-done(((bf16[2,3,80,512]{3,2,0,1:T(8,128)(2,1)}), bf16[64,3,80,512]{3,2,0,1:T(8,128)(2,1)}) %all-gather.6.cloned.1.call-update) | async-done | bytes 15728656 | tf_op jit(solution)/shard_map/all_gather | solution.py:323
  354.4 13.2 %copy.69 = bf16[64,3,80,512]{3,2,1,0:T(8,128)(2,1)} copy(bf16[64,3,80,512]{3,2,0,1:T(8,128)(2,1)} %all-gather.6.cloned.1.call-done) | data formatting | bytes 31457280 | tf_op jit(solution)/shard_map/all_gather | solution.py:323
  367.7 20.1 %sort_rows.6 = bf16[8192,320]{1,0:T(8,128)(2,1)} custom-call(s32[4096]{0:T(1024)} %bitcast.90, bf16[4096,320]{1,0:T(8,128)(2,1)} %token_layer.3.x_ref.refs_4_), custom_call_target="tpu_custom_call" | custom-call | flops 2000000000 | bytes 9000000 | tf_op jit(solution)/shard_map/sort_rows/pallas_call | solution.py:112
  387.8 77.5 %token_layer.4 = (bf16[4096,320]{1,0:T(8,128)(2,1)}, bf16[4096,320]{1,0:T(8,128)(2,1)}, f32[16,256]{1,0:T(8,128)}) custom-call(s32[4096]{0:T(1024)} %bitcast.91, s32[16]{0:T(128)} %get-tuple-element.83.cnt_ref, bf16[16,512,320]{2,1,0:T(8,128)(2,1)} %bitcast.68, bf16[16,512,320]{2,1,0:T(8,128)(2,1)} %bitcast.79, f32[32,256]{1,0:T(8,128)} %get-tuple-element.34.refs_2_, ...), custom_call_target="tpu_custom_call" | custom-call | flops 16106127360 | bytes 30000000 | tf_op jit(solution)/shard_map/token_layer/pallas_call | solution.py:255
  465.3 25.2 %sort_rows.9 = (bf16[8192,320]{1,0:T(8,128)(2,1)}, f32[32,256]{1,0:T(8,128)}) custom-call(s32[4096]{0:T(1024)} %bitcast.86, bf16[4096,320]{1,0:T(8,128)(2,1)} %get-tuple-element.37.x_ref.refs_5_, f32[16,256]{1,0:T(8,128)} %reshape.101.refs_3_.refs_0_), custom_call_target="tpu_custom_call" | custom-call | flops 2000000000 | bytes 9000000 | tf_op jit(solution)/shard_map/sort_rows/pallas_call | solution.py:112
  490.5 1.4 reshape.109
  491.8 18.9 %all-to-all-start = ((f32[8,4,256]{2,1,0:T(4,128)}), f32[8,4,256]{2,1,0:T(4,128)S(1)}, u32[]{:S(2)}, u32[]{:S(2)}) async-start(f32[8,4,256]{2,1,0:T(4,128)} %reshape.109), calls=%async_computation | async-start | bytes 65536 | tf_op jit(solution)/shard_map/all_to_all | solution.py:314
  510.8 8.2 copy.79
  519.0 5.1 all-to-all-start.2
  524.1 8.1 copy.84
  532.2 108.1 %all-to-all-done.2 = bf16[8,1024,320]{1,2,0:T(8,128)(2,1)} async-done(((bf16[8,1024,320]{1,2,0:T(8,128)(2,1)}), bf16[8,1024,320]{1,2,0:T(8,128)(2,1)}, u32[]{:S(2)}, u32[]{:S(2)}) %all-to-all-start.2) | async-done | bytes 5242912 | tf_op jit(solution)/shard_map/all_to_all | solution.py:314
  640.3 4.8 all-to-all-start.4
  645.2 1.2 copy.82.w2_ref
  646.3 2.3 copy.89.w2_ref
  649.6 8.1 copy.78
  657.7 8.1 copy.87
  665.9 2.8 copy.72.x_ref.refs_4_
  668.7 4.5 copy.90
  673.8 20.1 %sort_rows.8 = bf16[8192,320]{1,0:T(8,128)(2,1)} custom-call(s32[4096]{0:T(1024)} %bitcast.87, bf16[4096,320]{1,0:T(8,128)(2,1)} %copy.72.x_ref.refs_4_), custom_call_target="tpu_custom_call" | custom-call | flops 2000000000 | bytes 9000000 | tf_op jit(solution)/shard_map/sort_rows/pallas_call | solution.py:112
  694.9 8.1 copy.80
  703.0 25.2 %weight_grads.2 = (f32[2,320,512]{2,1,0:T(8,128)}, f32[2,320,512]{2,1,0:T(8,128)}, f32[2,512,320]{2,1,0:T(8,128)}) custom-call(s32[8,2]{1,0:T(8,128)} %copy.81.cnt_ref, bf16[8,2,512,320]{3,2,1,0:T(8,128)(2,1)} %bitcast.81, bf16[8,2,512,320]{3,2,1,0:T(8,128)(2,1)} %bitcast.82, f32[8,4,256]{2,1,0:T(4,128)} %copy-done.4, bf16[2,320,512]{2,1,0:T(8,128)(2,1)} %w1_ref.2, ...), custom_call_target="tpu_custom_call" | custom-call | flops 16106127360 | bytes 20000000 | tf_op jit(solution)/shard_map/weight_grads/pallas_call | solution.py:299
  728.2 2.9 copy.92
  731.1 30.0 %all-to-all-done.4 = bf16[8,1024,320]{1,2,0:T(8,128)(2,1)} async-done(((bf16[8,1024,320]{1,2,0:T(8,128)(2,1)}), bf16[8,1024,320]{1,2,0:T(8,128)(2,1)}, u32[]{:S(2)}, u32[]{:S(2)}) %all-to-all-start.4) | async-done | bytes 5242912 | tf_op jit(solution)/shard_map/all_to_all | solution.py:314
  761.2 8.1 copy.85
  769.3 26.1 %weight_grads.3 = (f32[2,320,512]{2,1,0:T(8,128)}, f32[2,320,512]{2,1,0:T(8,128)}, f32[2,512,320]{2,1,0:T(8,128)}) custom-call(s32[8,2]{1,0:T(8,128)} %copy.88.cnt_ref, bf16[8,2,512,320]{3,2,1,0:T(8,128)(2,1)} %bitcast.83, bf16[8,2,512,320]{3,2,1,0:T(8,128)(2,1)} %bitcast.80, f32[8,4,256]{2,1,0:T(4,128)} %copy-done.3, bf16[2,320,512]{2,1,0:T(8,128)(2,1)} %w1_ref.3, ...), custom_call_target="tpu_custom_call" | custom-call | flops 16106127360 | bytes 20000000 | tf_op jit(solution)/shard_map/weight_grads/pallas_call | solution.py:299
  795.4 2.9 copy.93
  798.3 13.2 %copy.73 = bf16[64,3,80,512]{3,2,1,0:T(8,128)(2,1)} copy(bf16[64,3,80,512]{3,2,0,1:T(8,128)(2,1)} %all-gather.8.cloned.1.call-done) | data formatting | bytes 31457280 | tf_op jit(solution)/shard_map/all_gather | solution.py:323
  811.5 57.2 %token_layer.5 = (bf16[4096,320]{1,0:T(8,128)(2,1)}, f32[16,256]{1,0:T(8,128)}) custom-call(s32[4096]{0:T(1024)} %bitcast.88, s32[16]{0:T(128)} %get-tuple-element.82.cnt_ref, bf16[16,512,320]{2,1,0:T(8,128)(2,1)} %bitcast.75, bf16[16,512,320]{2,1,0:T(8,128)(2,1)} %bitcast.77, f32[32,256]{1,0:T(8,128)} %get-tuple-element.39.refs_2_, ...), custom_call_target="tpu_custom_call" | custom-call | flops 13421772800 | bytes 30000000 | tf_op jit(solution)/shard_map/token_layer/pallas_call | solution.py:255
  868.8 4.5 copy.91
  (60 shorter events, 17.5 us)
Async XLA Ops:
  7.2 12.6 %copy-start.5 = (f32[4096,1]{0,1:T(1,128)S(1)}, f32[4096,1]{0,1:T(1,128)}, u32[]{:S(2)}) copy-start(f32[4096,1]{0,1:T(1,128)} %param.23) | copy-start | bytes 49156
  7.2 135.0 %all-gather.4.cloned.1.call-start = ((), (), s32[]{:S(2)}) async-start(), calls=%async_computation.6 | async-start | bytes 16220160 | tf_op jit(solution)/shard_map/all_gather | solution.py:323
  10.9 343.5 %all-gather.6.cloned.1.call-start = ((), (), s32[]{:S(2)}) async-start(), calls=%async_computation.7 | async-start | bytes 16220160 | tf_op jit(solution)/shard_map/all_gather | solution.py:323
  21.1 38.3 %copy-start = (bf16[4096,320]{0,1:T(8,128)(2,1)S(1)}, bf16[4096,320]{0,1:T(8,128)(2,1)}, u32[]{:S(2)}) copy-start(bf16[4096,320]{0,1:T(8,128)(2,1)} %param.18) | copy-start | bytes 7864324
  52.3 38.1 %all-to-all-start.3 = ((f32[8,4,256]{2,1,0:T(4,128)}), f32[8,4,256]{2,1,0:T(4,128)S(1)}, u32[]{:S(2)}, u32[]{:S(2)}) async-start(f32[8,4,256]{2,1,0:T(4,128)} %reshape.114), calls=%async_computation.3 | async-start | bytes 65536 | tf_op jit(solution)/shard_map/all_to_all | solution.py:314
  90.4 5.3 copy-start.6
  90.4 6.6 copy-start.2
  90.5 7.5 copy-start.8
  90.5 558.2 %copy-start.3 = (f32[8,4,256]{2,1,0:T(4,128)}, f32[8,4,256]{2,1,0:T(4,128)S(1)}, u32[]{:S(2)}) copy-start(f32[8,4,256]{2,1,0:T(4,128)S(1)} %all-to-all-done.3.g_ref) | copy-start | bytes 98308
  90.5 173.3 %all-to-all-start.1 = ((bf16[8,1024,320]{1,2,0:T(8,128)(2,1)}), bf16[8,1024,320]{1,2,0:T(8,128)(2,1)}, u32[]{:S(2)}, u32[]{:S(2)}) async-start(bf16[8,1024,320]{1,2,0:T(8,128)(2,1)} %copy.77), calls=%async_computation.1 | async-start | bytes 10485760 | tf_op jit(solution)/shard_map/all_to_all | solution.py:314
  95.7 702.6 %all-gather.8.cloned.1.call-start = ((), (), s32[]{:S(2)}) async-start(), calls=%async_computation.8 | async-start | bytes 16220160 | tf_op jit(solution)/shard_map/all_gather | solution.py:323
  155.6 47.0 %copy-start.1 = (bf16[2,512,320]{1,2,0:T(8,128)(2,1)S(1)}, bf16[2,512,320]{1,2,0:T(8,128)(2,1)}, u32[]{:S(2)}) copy-start(bf16[2,512,320]{1,2,0:T(8,128)(2,1)} %param.26) | copy-start | bytes 1966084
  263.8 228.0 %all-to-all-start.5 = ((bf16[8,1024,320]{1,2,0:T(8,128)(2,1)}), bf16[8,1024,320]{1,2,0:T(8,128)(2,1)}, u32[]{:S(2)}, u32[]{:S(2)}) async-start(bf16[8,1024,320]{1,2,0:T(8,128)(2,1)} %copy.86), calls=%async_computation.5 | async-start | bytes 10485760 | tf_op jit(solution)/shard_map/all_to_all | solution.py:314
  491.8 27.1 %all-to-all-start = ((f32[8,4,256]{2,1,0:T(4,128)}), f32[8,4,256]{2,1,0:T(4,128)S(1)}, u32[]{:S(2)}, u32[]{:S(2)}) async-start(f32[8,4,256]{2,1,0:T(4,128)} %reshape.109), calls=%async_computation | async-start | bytes 65536 | tf_op jit(solution)/shard_map/all_to_all | solution.py:314
  519.0 174.9 %copy-start.4 = (f32[8,4,256]{2,1,0:T(4,128)}, f32[8,4,256]{2,1,0:T(4,128)S(1)}, u32[]{:S(2)}) copy-start(f32[8,4,256]{2,1,0:T(4,128)S(1)} %all-to-all-done.g_ref) | copy-start | bytes 98308
  519.0 121.3 %all-to-all-start.2 = ((bf16[8,1024,320]{1,2,0:T(8,128)(2,1)}), bf16[8,1024,320]{1,2,0:T(8,128)(2,1)}, u32[]{:S(2)}, u32[]{:S(2)}) async-start(bf16[8,1024,320]{1,2,0:T(8,128)(2,1)} %copy.79), calls=%async_computation.2 | async-start | bytes 10485760 | tf_op jit(solution)/shard_map/all_to_all | solution.py:314
  640.3 120.8 %all-to-all-start.4 = ((bf16[8,1024,320]{1,2,0:T(8,128)(2,1)}), bf16[8,1024,320]{1,2,0:T(8,128)(2,1)}, u32[]{:S(2)}, u32[]{:S(2)}) async-start(bf16[8,1024,320]{1,2,0:T(8,128)(2,1)} %copy.84), calls=%async_computation.4 | async-start | bytes 10485760 | tf_op jit(solution)/shard_map/all_to_all | solution.py:314
  665.9 7.3 copy-start.7
  868.8 4.5 copy-start.9
Sparse Core Ops, SparseCore 0:
  11.5 130.6 all-gather.3
  145.6 208.7 all-gather.5
  357.3 152.8 all-gather.7
